TPU v7x, 32 devices: a whole 2x2x4 slice. The times are simulated.
32 devices in a mesh: row: 4 (over z), col: 8 (over y, x, core).
Axes of the slice: x: 2, y: 2, z: 4, core: 2. Of those that a mesh axis runs over, the one named last changes fastest.
Arguments:
- tokens: bfloat16 [2048, 2048], P(('row', 'col')), may hold values from -6 to 6
- timestep: int32 [1], replicated, may hold values from 0 to 999
- mod_weight: float32 [256, 2048], replicated, may hold values from -0.375 to 0.375
- qkv_weight: bfloat16 [3, 2048, 2048], P(None, None, 'col'), may hold values from -0.125 to 0.125
- attn_scale: float32 [16], P('col'), may hold values from 4 to 40
- out_weight: bfloat16 [2048, 2048], P('col'), may hold values from -0.5 to 0.5
- grad_update: bfloat16 [2048, 2048], P(('row', 'col')), may hold values from -6 to 6
Outputs:
- update: bfloat16 [2048, 2048], P(('row', 'col'))
- grad_tokens: bfloat16 [2048, 2048], P(('row', 'col'))
- grad_qkv: float32 [3, 2048, 2048], P(None, 'row', 'col')
- grad_out: float32 [2048, 2048], P('col', 'row')
All inputs are finite; a program needn't handle non-finite values.
Results may differ from a plain program's by a relative error of at most 0.018.
Values may be sent and summed in bfloat16 or wider, within the bound.
A program may use at most 128 MiB of HBM per device.

v0:
```python
import math

import jax
import jax.numpy as jnp
from jax import lax
from jax.sharding import PartitionSpec as P

epsilon = 1e-06


def embed(timestep, count):
    index = jnp.arange(count, dtype=jnp.float32)
    freqs = jnp.exp(-math.log(10000.0) * index / count)
    angles = timestep.astype(jnp.float32)[0] * freqs
    return jnp.concatenate([jnp.cos(angles), jnp.sin(angles)])


def unit_rows(values):
    factor = lax.rsqrt(jnp.mean(values * values, -1, keepdims=True) + epsilon)
    return (values * factor, factor)


def unit_grad(grad_unit, unit, factor):
    return factor * (grad_unit - unit * jnp.mean(grad_unit * unit, -1, keepdims=True))


def split_blocks(array, size):
    return array.reshape((array.shape[0] // size, size) + array.shape[1:])


def per_device(tokens, timestep, mod_weight, qkv_weight, attn_scale, out_weight, grad_update):
    tok_dev, width = tokens.shape
    heads_here = attn_scale.shape[0]
    inner = qkv_weight.shape[2]
    head_dim = inner // heads_here
    span = tok_dev * lax.axis_size("col")
    coeff = attn_scale / head_dim
    embedded = embed(timestep, mod_weight.shape[0] // 2)
    gain = 1.0 + jnp.sum(embedded[:, None] * mod_weight, 0)
    tok_float = tokens.astype(jnp.float32)
    rstd = lax.rsqrt(jnp.mean(tok_float * tok_float, -1, keepdims=True) + epsilon)
    normed = tok_float * rstd
    hidden = (normed * gain).astype(jnp.bfloat16)
    group = lax.all_gather(hidden, "col", axis=0, tiled=True)
    raw = jnp.einsum("sd,kdh->ksh", group, qkv_weight, preferred_element_type=jnp.float32)
    query_unit, query_factor = unit_rows(raw[0].reshape(span, heads_here, head_dim))
    key_unit, key_factor = unit_rows(raw[1].reshape(span, heads_here, head_dim))
    queries = query_unit.astype(jnp.bfloat16)
    key_heads = key_unit.astype(jnp.bfloat16)
    value_heads = raw[2].astype(jnp.bfloat16).reshape(span, heads_here, head_dim)
    start_state = (
        jnp.zeros((heads_here, span), jnp.float32),
        jnp.zeros((span, heads_here, head_dim), jnp.float32),
    )
    carry = start_state
    key_piece = lax.all_gather(key_heads, "row", axis=0, tiled=True)
    value_piece = lax.all_gather(value_heads, "row", axis=0, tiled=True)
    size = math.gcd(key_piece.shape[0], 512)

    def attend_step(state, block):
        key_block, value_block = block
        scores = (
            jnp.einsum("qhd,khd->hqk", queries, key_block, preferred_element_type=jnp.float32)
            * coeff[:, None, None]
        )
        weights = jnp.exp(scores - attn_scale[:, None, None])
        totals = state[0] + jnp.sum(weights, -1)
        mixed = state[1] + jnp.einsum(
            "hqk,khd->qhd",
            weights.astype(jnp.bfloat16),
            value_block,
            preferred_element_type=jnp.float32,
        )
        return ((totals, mixed), None)

    carry, unused = lax.scan(
        attend_step, carry, (split_blocks(key_piece, size), split_blocks(value_piece, size))
    )
    totals, mixed = carry
    attended_heads = (mixed / totals.T[:, :, None]).astype(jnp.bfloat16)
    attended = attended_heads.reshape(span, inner)
    rows = attended
    update = lax.psum_scatter(
        jnp.dot(rows, out_weight, preferred_element_type=jnp.float32).astype(jnp.bfloat16),
        "col",
        scatter_dimension=0,
        tiled=True,
    )
    grad_group = lax.all_gather(grad_update, "col", axis=0, tiled=True)
    out_part = lax.dot_general(
        attended, grad_group, (((0,), (0,)), ((), ())), preferred_element_type=jnp.float32
    )
    grad_out = lax.psum_scatter(
        out_part.astype(jnp.bfloat16), "row", scatter_dimension=1, tiled=True
    ).astype(jnp.float32)
    grad_attended = lax.dot_general(
        grad_group, out_weight, (((1,), (1,)), ((), ())), preferred_element_type=jnp.float32
    ).astype(jnp.bfloat16)
    grad_heads = grad_attended.reshape(span, heads_here, head_dim)
    delta = jnp.sum(grad_heads.astype(jnp.float32) * attended_heads.astype(jnp.float32), -1)
    inverse = 1.0 / totals

    def pair_terms(query_rows, grad_rows, inverse_rows, delta_rows, key_block, value_block):
        scores = (
            jnp.einsum("qhd,khd->hqk", query_rows, key_block, preferred_element_type=jnp.float32)
            * coeff[:, None, None]
        )
        probs = jnp.exp(scores - attn_scale[:, None, None]) * inverse_rows[:, :, None]
        dprobs = jnp.einsum(
            "qhd,khd->hqk", grad_rows, value_block, preferred_element_type=jnp.float32
        )
        dscores = (probs * (dprobs - delta_rows[:, :, None]) * coeff[:, None, None]).astype(
            jnp.bfloat16
        )
        return (probs, dscores)

    empty_own = jnp.zeros((span, heads_here, head_dim), jnp.float32)
    carry = empty_own
    key_piece = lax.all_gather(key_heads, "row", axis=0, tiled=True)
    value_piece = lax.all_gather(value_heads, "row", axis=0, tiled=True)
    size = math.gcd(key_piece.shape[0], 512)

    def query_step(state, block):
        key_block, value_block = block
        probs, dscores = pair_terms(queries, grad_heads, inverse, delta.T, key_block, value_block)
        return (
            state
            + jnp.einsum("hqk,khd->qhd", dscores, key_block, preferred_element_type=jnp.float32),
            None,
        )

    carry, unused = lax.scan(
        query_step, carry, (split_blocks(key_piece, size), split_blocks(value_piece, size))
    )
    grad_query = carry
    all_inverse, all_delta = (
        lax.all_gather(inverse.T, "row", axis=0, tiled=True),
        lax.all_gather(delta, "row", axis=0, tiled=True),
    )
    carry = (empty_own, empty_own)
    query_piece = lax.all_gather(queries, "row", axis=0, tiled=True)
    grad_piece = lax.all_gather(grad_heads, "row", axis=0, tiled=True)
    count = query_piece.shape[0]
    size = math.gcd(count, 512)

    def key_step(state, block):
        query_block, grad_block, inverse_block, delta_block = block
        probs, dscores = pair_terms(
            query_block, grad_block, inverse_block.T, delta_block.T, key_heads, value_heads
        )
        grad_key = state[0] + jnp.einsum(
            "hqk,qhd->khd", dscores, query_block, preferred_element_type=jnp.float32
        )
        grad_value = state[1] + jnp.einsum(
            "hqk,qhd->khd",
            probs.astype(jnp.bfloat16),
            grad_block,
            preferred_element_type=jnp.float32,
        )
        return ((grad_key, grad_value), None)

    carry, unused = lax.scan(
        key_step,
        carry,
        (
            split_blocks(query_piece, size),
            split_blocks(grad_piece, size),
            split_blocks(all_inverse, size),
            split_blocks(all_delta, size),
        ),
    )
    grad_key, grad_value = carry
    grad_q = (
        unit_grad(grad_query, query_unit, query_factor).astype(jnp.bfloat16).reshape(span, inner)
    )
    grad_k = unit_grad(grad_key, key_unit, key_factor).astype(jnp.bfloat16).reshape(span, inner)
    grad_v = grad_value.astype(jnp.bfloat16).reshape(span, inner)
    grad_raw = jnp.stack([grad_q, grad_k, grad_v])
    qkv_part = jnp.einsum("sd,ksh->kdh", group, grad_raw, preferred_element_type=jnp.float32)
    grad_qkv = lax.psum_scatter(
        qkv_part.astype(jnp.bfloat16), "row", scatter_dimension=1, tiled=True
    ).astype(jnp.float32)
    rows = grad_raw
    grad_hidden = lax.psum_scatter(
        jnp.einsum("ksh,kdh->sd", rows, qkv_weight, preferred_element_type=jnp.float32).astype(
            jnp.bfloat16
        ),
        "col",
        scatter_dimension=0,
        tiled=True,
    ).astype(jnp.float32)
    grad_normed = grad_hidden * gain
    grad_tokens = (
        rstd * (grad_normed - normed * jnp.mean(grad_normed * normed, -1, keepdims=True))
    ).astype(jnp.bfloat16)
    return (update, grad_tokens, grad_qkv, grad_out)


def solution(mesh):
    placed = (
        P(("row", "col"), None),
        P(),
        P(),
        P(None, None, "col"),
        P("col"),
        P("col", None),
        P(("row", "col"), None),
    )
    return jax.shard_map(
        per_device,
        mesh=mesh,
        in_specs=placed,
        out_specs=(
            P(("row", "col"), None),
            P(("row", "col"), None),
            P(None, "row", "col"),
            P("col", "row"),
        ),
        check_vma=False,
    )
```

profile of v0, /device:TPU:0, one launch (start us, length us, event | category | flops | bytes accessed | tf_op | source)
XLA Modules:
  0.0 422.1 jit_solution(2159010349905390229)
XLA Ops:
  8.1 1.9 multiply_reduce_fusion
  11.1 30.6 %all-gather.7.cloned.1.call-done = bf16[512,2048]{1,0:T(8,128)(2,1)} async-done(((bf16[64,2048]{1,0:T(8,128)(2,1)}), bf16[512,2048]{1,0:T(8,128)(2,1)}) %all-gather.7.cloned.1.call-update) | async-done | bytes 2097168 | tf_op jit(solution)/shard_map/all_gather | solution.py:44
  41.7 3.4 fusion.54
  48.8 1.8 slice.17
  51.3 1.8 copy.43
  53.1 1.8 copy.45
  54.9 2.0 copy.31
  60.4 16.5 %all-gather.9.cloned.1.call-done = bf16[2048,2,128]{0,2,1:T(8,128)(2,1)} async-done(((bf16[512,2,128]{0,2,1:T(8,128)(2,1)}), bf16[2048,2,128]{0,2,1:T(8,128)(2,1)}) %all-gather.9.cloned.1.call-update) | async-done | bytes 1048592 | tf_op jit(solution)/shard_map/all_gather | solution.py:56
  76.9 2.6 reshape.88
  79.5 2.7 copy.33
  82.3 23.6 %all-gather.11.cloned.1.call-done = bf16[2048,2,128]{0,2,1:T(8,128)(2,1)} async-done(((bf16[512,2,128]{0,2,1:T(8,128)(2,1)}), bf16[2048,2,128]{0,2,1:T(8,128)(2,1)}) %all-gather.11.cloned.1.call-update) | async-done | bytes 1048592 | tf_op jit(solution)/shard_map/all_gather | solution.py:57
  105.9 3.7 copy.32
  109.5 32.0 %while.37 = (s32[]{:T(128)}, f32[2,512]{1,0:T(2,128)S(1)}, f32[512,2,128]{0,2,1:T(8,128)}, bf16[4,512,2,128]{3,1,2,0:T(8,128)(2,1)}, bf16[512,2,128]{2,0,1:T(8,1...) while((s32[]{:T(128)}, f32[2,512]{1,0:T(2,128)S(1)}, ...), condition=%wide.region_6.7_spmd.clone, body=%wide.region_4.6_spmd.clone.sunk | while | flops 271844352 | bytes 8143544 | solution.py:76
  109.5 2.8 bitcast_reduce_fusion.2
  114.3 3.2 fusion.103
  117.5 2.8 bitcast_reduce_fusion.2
  122.3 3.2 fusion.103
  125.5 2.8 bitcast_reduce_fusion.2
  130.3 3.2 fusion.103
  133.5 2.8 bitcast_reduce_fusion.2
  138.3 3.2 fusion.103
  141.5 3.5 multiply_reduce_fusion.3
  145.1 1.9 copy.37
  147.0 1.8 copy.41
  148.8 2.4 copy.76
  151.2 33.2 %while.38 = (s32[]{:T(128)}, f32[512,2,128]{0,2,1:T(8,128)}, bf16[4,512,2,128]{1,3,2,0:T(8,128)(2,1)}, bf16[512,2,128]{2,1,0:T(2,128)(2,1)S(1)}, f32[2]{0:T(128)...) while((s32[]{:T(128)}, f32[512,2,128]{0,2,1:T(8,128)}, ...), condition=%wide.region_10.11_spmd.clone, body=%wide.region_9.10_spmd.clone.sunk | while | flops 406585344 | bytes 7087251 | solution.py:132
  151.2 2.8 fusion.109
  154.0 1.8 dynamic-slice_bitcast_fusion.5
  155.9 3.6 fusion.110
  159.5 2.8 fusion.109
  162.3 1.8 dynamic-slice_bitcast_fusion.5
  164.1 3.6 fusion.110
  167.8 2.8 fusion.109
  170.6 1.8 dynamic-slice_bitcast_fusion.5
  172.4 3.8 fusion.110
  176.2 2.8 fusion.109
  179.0 1.8 dynamic-slice_bitcast_fusion.5
  180.8 3.6 fusion.110
  184.4 2.0 copy.39
  190.8 13.2 %all_gather.33 = f32[2048,2]{0,1:T(2,128)S(1)} all-gather(f32[512,2]{0,1:T(2,128)S(1)} %get-tuple-element.734), channel_id=1, replica_groups=mesh['row'=4,'col'=8] {'row'}, dimensions={0}, use_global_device_ids=true | all-gather | bytes 20480 | tf_op jit(solution)/shard_map/all_gather | solution.py:138
  204.0 13.2 %all_gather.31 = f32[2048,2]{0,1:T(2,128)S(1)} all-gather(f32[512,2]{0,1:T(2,128)S(1)} %fusion.81), channel_id=1, replica_groups=mesh['row'=4,'col'=8] {'row'}, dimensions={0}, use_global_device_ids=true | all-gather | bytes 20480 | tf_op jit(solution)/shard_map/all_gather | solution.py:137
  217.2 3.4 convolution_convert_fusion.2
  220.9 36.4 %while.39 = (s32[]{:T(128)}, f32[512,2,128]{0,2,1:T(8,128)}, f32[512,2,128]{0,2,1:T(8,128)}, bf16[4,512,2,128]{3,1,0,2:T(8,128)(2,1)}, bf16[512,2,128]{2,0,1:T(8...) while((s32[]{:T(128)}, f32[512,2,128]{0,2,1:T(8,128)}, ...), condition=%wide.region_13.14_spmd.clone, body=%wide.region_12.13_spmd.clone.sunk | while | flops 541589504 | bytes 9988260 | solution.py:162
  221.0 2.9 exponential_multiply_fusion.3
  223.9 2.8 fusion.119
  226.7 3.2 fusion.118
  230.0 2.9 exponential_multiply_fusion.3
  232.8 2.9 fusion.119
  235.8 3.3 fusion.118
  239.1 2.9 exponential_multiply_fusion.3
  242.0 2.9 fusion.119
  244.9 3.3 fusion.118
  248.2 2.9 exponential_multiply_fusion.3
  251.1 2.9 fusion.119
  254.0 3.3 fusion.118
  262.7 4.3 %bitcast_convert_fusion.2 = bf16[512,2048]{1,0:T(8,128)(2,1)} fusion(bf16[3,2048,256]{2,1,0:T(8,128)(2,1)S(1)} %copy-done, bf16[1,512,256]{2,1,0:T(8,128)(2,1)} %copy.59, bf16[1,512,256]{2,1,0:T(8,128)(2,1)} %copy.58, bf16[1,512,256]{2,1,0:T(8,128)(2,1)} %stack_reshape.9), kind=kOutput, calls=%fused_computation.57 | convolution fusion | flops 1612447744 | bytes 6029312 | tf_op jit(solution)/shard_map/ksh,kdh->sd/dot_general | solution.py:185
  268.0 5.2 %fusion.50 = bf16[3,2048,256]{1,2,0:T(8,128)(2,1)} fusion(bf16[512,2048]{1,0:T(8,128)(2,1)} %all-gather.7.cloned.1.call-done, bf16[1,512,256]{2,1,0:T(8,128)(2,1)} %copy.59, bf16[1,512,256]{2,1,0:T(8,128)(2,1)} %copy.58, bf16[1,512,256]{2,1,0:T(8,128)(2,1)S(1)} %copy-done.11), kind=kOutput, calls=%fused_computation.60 | convolution fusion | flops 1612972032 | bytes 6029312 | tf_op jit(solution)/shard_map/sd,ksh->kdh/dot_general | solution.py:179
  274.2 3.4 convolution_convert_fusion.1
  277.6 1.8 convert_element_type.101
  279.5 28.2 %reduce-scatter.7.cloned.1.call-done = bf16[64,2048]{1,0:T(8,128)(2,1)} async-done(((bf16[512,2048]{1,0:T(8,128)(2,1)}), bf16[64,2048]{1,0:T(8,128)(2,1)}) %reduce-scatter.7.cloned.1.call-update) | async-done | bytes 262160 | tf_op jit(solution)/shard_map/reduce_scatter | solution.py:184
  308.9 1.8 fusion.64
  310.8 59.7 %reduce-scatter.9.cloned.1.call-done = bf16[3,512,256]{1,2,0:T(8,128)(2,1)} async-done(((bf16[3,2048,256]{1,2,0:T(8,128)(2,1)}), bf16[3,512,256]{1,2,0:T(8,128)(2,1)}) %reduce-scatter.9.cloned.1.call-update) | async-done | bytes 786448 | tf_op jit(solution)/shard_map/reduce_scatter | solution.py:180
  370.5 2.5 copy.49
  373.0 42.2 %reduce-scatter.5.cloned.1.call-done = bf16[64,2048]{1,0:T(8,128)(2,1)} async-done(((bf16[512,2048]{1,0:T(8,128)(2,1)}), bf16[64,2048]{1,0:T(8,128)(2,1)}) %reduce-scatter.5.cloned.1.call-update) | async-done | bytes 262160 | tf_op jit(solution)/shard_map/reduce_scatter | solution.py:83
  (107 shorter events, 30.1 us)
Async XLA Ops:
  7.2 34.6 %copy-start = (bf16[3,2048,256]{2,1,0:T(8,128)(2,1)S(1)}, bf16[3,2048,256]{2,1,0:T(8,128)(2,1)}, u32[]{:S(2)}) copy-start(bf16[3,2048,256]{2,1,0:T(8,128)(2,1)} %param.16) | copy-start | bytes 9437188
  7.2 2.9 copy-start.7
  7.2 34.5 %all-gather.7.cloned.1.call-start = ((), (), s32[]{:S(2)}) async-start(), calls=%async_computation.4 | async-start | bytes 2359296 | tf_op jit(solution)/shard_map/all_gather | solution.py:44
  11.1 65.8 %all-gather.9.cloned.1.call-start = ((), (), s32[]{:S(2)}) async-start(), calls=%async_computation.5 | async-start | bytes 1310720 | tf_op jit(solution)/shard_map/all_gather | solution.py:56
  45.2 1.1 copy-start.10
  46.3 5.0 %copy-start.12 = (f32[2]{0:T(128)S(1)}, f32[2]{0:T(128)}, u32[]{:S(2)}) copy-start(f32[2]{0:T(128)} %param.17) | copy-start | bytes 28
  47.2 0.8 copy-start.4
  48.8 57.1 %all-gather.11.cloned.1.call-start = ((), (), s32[]{:S(2)}) async-start(), calls=%async_computation.6 | async-start | bytes 1310720 | tf_op jit(solution)/shard_map/all_gather | solution.py:57
  50.6 90.9 %all-gather.13.cloned.1.call-start = ((), (), s32[]{:S(2)}) async-start(), calls=%async_computation.8 | async-start | bytes 2359296 | tf_op jit(solution)/shard_map/all_gather | solution.py:89
  51.2 169.7 %all-gather.15.cloned.1.call-start = ((), (), s32[]{:S(2)}) async-start(), calls=%async_computation.9 | async-start | bytes 1310720 | tf_op jit(solution)/shard_map/all_gather | solution.py:141
  59.4 1.0 copy-start.1
  60.4 160.5 %all-gather.17.cloned.1.call-start = ((), (), s32[]{:S(2)}) async-start(), calls=%async_computation.10 | async-start | bytes 1310720 | tf_op jit(solution)/shard_map/all_gather | solution.py:142
  79.5 30.0 %copy-start.2 = (bf16[512,2,128]{2,0,1:T(8,128)(2,1)S(1)}, bf16[512,2,128]{2,0,1:T(8,128)(2,1)}, u32[]{:S(2)}) copy-start(bf16[512,2,128]{2,0,1:T(8,128)(2,1)} %copy-done.1) | copy-start | bytes 786436
  114.3 3.2 copy-start.3
  122.3 3.2 copy-start.3
  130.3 3.2 copy-start.3
  138.3 3.2 copy-start.3
  145.1 6.1 %copy-start.6 = (bf16[512,2,128]{2,1,0:T(2,128)(2,1)S(1)}, bf16[512,2,128]{2,1,0:T(2,128)(2,1)}, u32[]{:S(2)}) copy-start(bf16[512,2,128]{2,1,0:T(2,128)(2,1)} %copy.36) | copy-start | bytes 786436
  151.2 126.4 %reduce-scatter.11.cloned.1.call-start = ((), (), s32[]{:S(2)}) async-start(), calls=%async_computation.13 | async-start | bytes 1310720 | tf_op jit(solution)/shard_map/reduce_scatter | solution.py:93
  217.2 3.7 copy-start.5
  220.7 87.1 %reduce-scatter.7.cloned.1.call-start = ((), (), s32[]{:S(2)}) async-start(), calls=%async_computation.11 | async-start | bytes 2359296 | tf_op jit(solution)/shard_map/reduce_scatter | solution.py:184
  267.0 0.9 copy-start.11
  267.1 103.4 %reduce-scatter.9.cloned.1.call-start = ((), (), s32[]{:S(2)}) async-start(), calls=%async_computation.12 | async-start | bytes 3932160 | tf_op jit(solution)/shard_map/reduce_scatter | solution.py:180
  273.2 1.0 copy-start.9
  273.3 142.0 %reduce-scatter.5.cloned.1.call-start = ((), (), s32[]{:S(2)}) async-start(), calls=%async_computation.7 | async-start | bytes 2359296 | tf_op jit(solution)/shard_map/reduce_scatter | solution.py:83
  277.6 30.2 %copy-start.8 = (bf16[64,2048]{1,0:T(8,128)(2,1)S(1)}, bf16[64,2048]{1,0:T(8,128)(2,1)}, u32[]{:S(2)}) copy-start(bf16[64,2048]{1,0:T(8,128)(2,1)} %param.13) | copy-start | bytes 786436
Sparse Core Ops, SparseCore 0:
  11.2 30.4 all-gather.6
  48.9 27.9 all-gather.8
  78.5 27.3 all-gather.10
  107.6 27.1 all-gather.12
  136.8 28.0 all-gather.14
  166.3 27.3 all-gather.16
  220.8 26.5 reduce-scatter.10
  267.2 40.4 reduce-scatter.6
  310.0 60.3 reduce-scatter.8
  374.2 41.0 reduce-scatter.4
where the time goes:
time: 424 us; the launch traced here: 422 us
  waiting for transfers between devices  202 us (48%)
  matrix products  109 us (26%)
  local copies, waits for them, and re-layouts  50.9 us (12%)
  blocking collectives  26.4 us (6%)
  other arithmetic  17.9 us (4%)
  between operations  15.3 us (4%)
    reduce_scatter x1, waiting for transfers between devices, per_device(): lax.psum_scatter(qkv_part.astype(jnp.bfloat16), 'row', scatter_dimension=...  59.7 us
    reduce_scatter x1, waiting for transfers between devices, per_device(): lax.psum_scatter(jnp.dot(rows, out_weight, preferred_element_type=jnp.flo...  42.2 us
    all_gather x1, waiting for transfers between devices, per_device(): group = lax.all_gather(hidden, 'col', axis=0, tiled=True)  30.6 us
    reduce_scatter x1, waiting for transfers between devices, per_device(): lax.psum_scatter(jnp.einsum('ksh,kdh->sd', rows, qkv_weight, preferred_el...  28.2 us
    all_gather x1, waiting for transfers between devices, per_device(): value_piece = lax.all_gather(value_heads, 'row', axis=0, tiled=True)  23.6 us
    dot_general x8, matrix products, pair_terms(): jnp.einsum('qhd,khd->hqk', query_rows, key_block, preferred_element_type=...  22.8 us
    all_gather x1, waiting for transfers between devices, per_device(): key_piece = lax.all_gather(key_heads, 'row', axis=0, tiled=True)  16.5 us
    unnamed x30, local copies, waits for them, and re-layouts  15.4 us
  transfers between devices with their start and end apart: 10, of which 6 were waited for; matrix products, arithmetic and copies ran while one was open for 39% of the time, Pallas kernels for 0%

commit v1 on v0

v1 whole, which is shorter than its diff:
```python
import functools
import math

import jax
import jax.numpy as jnp
from jax import lax
from jax.experimental import pallas as pl
from jax.experimental.pallas import tpu as pltpu
from jax.sharding import PartitionSpec as P

epsilon = 1e-06
MESH = pl.DeviceIdType.MESH
RELAYED = 4


def embed(timestep, count):
    index = jnp.arange(count, dtype=jnp.float32)
    freqs = jnp.exp(-math.log(10000.0) * index / count)
    angles = timestep.astype(jnp.float32)[0] * freqs
    return jnp.concatenate([jnp.cos(angles), jnp.sin(angles)])


def by_head(array, head_dim):
    return [array[:, at : at + head_dim] for at in range(0, array.shape[1], head_dim)]


def unit_rows(values):
    factor = lax.rsqrt(jnp.mean(values * values, -1, keepdims=True) + epsilon)
    return (values * factor, factor)


def unit_grad(grad_unit, unit, factor):
    return factor * (grad_unit - unit * jnp.mean(grad_unit * unit, -1, keepdims=True))


def piece(ref, dim, size, index):
    start = index * size
    if dim == len(ref.shape) - 1:
        start = pl.multiple_of(start, 128)
    elif dim == len(ref.shape) - 2:
        start = pl.multiple_of(start, 16)
    return ref.at[(slice(None),) * dim + (pl.ds(start, size),)]


def half(ref, side):
    dim = len(ref.shape) - 2
    size = ref.shape[dim] // 2
    return ref.at[(slice(None),) * dim + (pl.ds(side * size, size),)]


def exchange_kernel(plan, *refs):
    count = len(plan)
    sources, targets = refs[:count], refs[count : 2 * count]
    own_sem, send_sem, recv_sem = refs[2 * count : 2 * count + 3]
    relays = refs[2 * count + 3 :]
    sizes = {axis: n for axis, n, dim, size in plan}
    barrier = pltpu.get_barrier_semaphore()
    for axis, n in sizes.items():
        me = lax.axis_index(axis)
        for step in range(1, n):
            pl.semaphore_signal(
                barrier, inc=1, device_id={axis: lax.rem(me + step, n)}, device_id_type=MESH
            )
    pl.semaphore_wait(barrier, sum(n - 1 for n in sizes.values()))
    def send(job, slot, source, target, peer):
        copy = pltpu.make_async_remote_copy(
            src_ref=source,
            dst_ref=target,
            send_sem=send_sem.at[job, slot],
            recv_sem=recv_sem.at[job, slot],
            device_id={plan[job][0]: peer},
            device_id_type=MESH,
        )
        copy.start()
        return copy

    copies, hops = [], {}
    relayed = [job for job in range(count) if plan[job][1] == RELAYED]
    for job in relayed:
        axis, n, dim, size = plan[job]
        if dim is None:
            continue
        me = lax.axis_index(axis)
        right, left = lax.rem(me + 1, n), lax.rem(me + 3, n)
        opposite = piece(sources[job], dim, size, lax.rem(me + 2, n))
        first = send(job, 4, half(opposite, 0), relays[job].at[0], right)
        second = send(job, 5, half(opposite, 1), relays[job].at[1], left)
        hops[job] = (first, second)
    for step in range(1, max(sizes.values())):
        for job, (axis, n, dim, size) in enumerate(plan):
            if step >= n or (n == RELAYED and step == 2):
                continue
            me = lax.axis_index(axis)
            peer = lax.rem(me + step, n)
            source = sources[job]
            source = source if dim is None else piece(source, dim, size, peer)
            copy = send(job, step, source, targets[job].at[me], peer)
            if n == RELAYED and dim is None:
                hops.setdefault(job, []).append(copy)
            else:
                copies.append(copy)
    for job, (axis, n, dim, size) in enumerate(plan):
        me = lax.axis_index(axis)
        source = sources[job]
        copy = pltpu.make_async_copy(
            source if dim is None else piece(source, dim, size, me),
            targets[job].at[me],
            own_sem.at[job],
        )
        copy.start()
        copies.append(copy)
    for side in range(2):
        for job in relayed:
            axis, n, dim, size = plan[job]
            me = lax.axis_index(axis)
            right, left = lax.rem(me + 1, n), lax.rem(me + 3, n)
            onward, origin = (right, left) if side == 0 else (left, right)
            hops[job][side].wait_recv()
            landing = half(targets[job].at[origin], side)
            source = landing if dim is None else relays[job].at[side]
            copies.append(send(job, 6 + side, source, landing, onward))
    for job in relayed:
        for copy in hops[job]:
            copy.wait_send()
    for copy in copies:
        copy.wait()


def exchange(jobs, collective_id):
    plan, shapes, relays = [], [], []
    for array, axis, dim in jobs:
        n = lax.axis_size(axis)
        block = list(array.shape)
        size = None
        if dim is not None:
            size = block[dim] = block[dim] // n
        plan.append((axis, n, dim, size))
        shapes.append(jax.ShapeDtypeStruct((n,) + tuple(block), array.dtype))
        if n == RELAYED and dim is not None:
            block[-2] //= 2
        else:
            block = [16, 128]
        relays.append(pltpu.VMEM((2,) + tuple(block), array.dtype))
    most = max(2 * RELAYED, max(n for axis, n, dim, size in plan))
    count = len(jobs)
    in_vmem = pl.BlockSpec(memory_space=pltpu.VMEM)
    return pl.pallas_call(
        functools.partial(exchange_kernel, tuple(plan)),
        out_shape=shapes,
        in_specs=[in_vmem] * count,
        out_specs=[in_vmem] * count,
        scratch_shapes=[
            pltpu.SemaphoreType.DMA((count,)),
            pltpu.SemaphoreType.DMA((count, most)),
            pltpu.SemaphoreType.DMA((count, most)),
            *relays,
        ],
        compiler_params=pltpu.CompilerParams(
            collective_id=collective_id, has_side_effects=True, vmem_limit_bytes=48 * 2**20
        ),
        name=f"exchange_{collective_id}",
    )(*[array for array, axis, dim in jobs])


def dot_rows(left, right):
    return lax.dot_general(
        left, right, (((1,), (1,)), ((), ())), preferred_element_type=jnp.float32
    )


def dot_columns(left, right):
    return lax.dot_general(
        left, right, (((0,), (0,)), ((), ())), preferred_element_type=jnp.float32
    )


def attention_kernel(
    scale_ref, q_ref, k_ref, v_ref, g_ref, o_ref, dq_ref, dk_ref, dv_ref, dk_sum, dv_sum
):
    block = pl.program_id(1)
    scale = scale_ref[pl.program_id(0)]
    coeff = scale * (1.0 / q_ref.shape[1])
    query, keys, values, grad = q_ref[...], k_ref[...], v_ref[...], g_ref[...]
    weights = jnp.exp(dot_rows(query, keys) * coeff - scale)
    inverse = 1.0 / jnp.sum(weights, -1, keepdims=True)
    mixed = jnp.dot(weights.astype(jnp.bfloat16), values, preferred_element_type=jnp.float32)
    attended = (mixed * inverse).astype(jnp.bfloat16)
    o_ref[...] = attended
    delta = jnp.sum(
        grad.astype(jnp.float32) * attended.astype(jnp.float32), -1, keepdims=True
    )
    probs = weights * inverse
    dscores = (probs * (dot_rows(grad, values) - delta) * coeff).astype(jnp.bfloat16)
    dq_ref[...] = jnp.dot(dscores, keys, preferred_element_type=jnp.float32)
    dk_part = dot_columns(dscores, query)
    dv_part = dot_columns(probs.astype(jnp.bfloat16), grad)

    @pl.when(block == 0)
    def _():
        dk_sum[...] = dk_part
        dv_sum[...] = dv_part

    @pl.when(block > 0)
    def _():
        dk_sum[...] += dk_part
        dv_sum[...] += dv_part

    @pl.when(block == pl.num_programs(1) - 1)
    def _():
        dk_ref[...] = dk_sum[...].astype(jnp.bfloat16)
        dv_ref[...] = dv_sum[...].astype(jnp.bfloat16)


def attention(attn_scale, queries, keys_values, grads):
    heads = attn_scale.shape[0]
    span, inner = queries.shape
    length = keys_values.shape[0]
    head_dim = inner // heads
    size = math.gcd(span, 256)
    while size * length > 2**19 and size % 32 == 0:
        size //= 2
    mine = pl.BlockSpec((size, head_dim), lambda h, i: (i, h))
    keys = pl.BlockSpec((length, head_dim), lambda h, i: (0, h))
    values = pl.BlockSpec((length, head_dim), lambda h, i: (0, heads + h))
    return pl.pallas_call(
        attention_kernel,
        grid=(heads, span // size),
        out_shape=[
            jax.ShapeDtypeStruct((span, inner), jnp.bfloat16),
            jax.ShapeDtypeStruct((span, inner), jnp.float32),
            jax.ShapeDtypeStruct((length, inner), jnp.bfloat16),
            jax.ShapeDtypeStruct((length, inner), jnp.bfloat16),
        ],
        in_specs=[pl.BlockSpec(memory_space=pltpu.SMEM), mine, keys, values, mine],
        out_specs=[mine, mine, keys, keys],
        scratch_shapes=[pltpu.VMEM((length, head_dim), jnp.float32)] * 2,
        compiler_params=pltpu.CompilerParams(
            dimension_semantics=("arbitrary", "arbitrary"), vmem_limit_bytes=56 * 2**20
        ),
        name="attention",
    )(attn_scale, queries, keys_values, keys_values, grads)


def add_up(slots):
    return jnp.sum(slots.astype(jnp.float32), 0)


def per_device(tokens, timestep, mod_weight, qkv_weight, attn_scale, out_weight, grad_update):
    tok_dev, width = tokens.shape
    heads_here = attn_scale.shape[0]
    inner = qkv_weight.shape[2]
    head_dim = inner // heads_here
    span = tok_dev * lax.axis_size("col")
    embedded = embed(timestep, mod_weight.shape[0] // 2)
    gain = 1.0 + jnp.sum(embedded[:, None] * mod_weight, 0)
    tok_float = tokens.astype(jnp.float32)
    rstd = lax.rsqrt(jnp.mean(tok_float * tok_float, -1, keepdims=True) + epsilon)
    normed = tok_float * rstd
    hidden = (normed * gain).astype(jnp.bfloat16)
    (group,) = exchange([(hidden, "col", None)], 0)
    group = group.reshape(span, width)
    raw = [jnp.dot(group, qkv_weight[k], preferred_element_type=jnp.float32) for k in range(3)]
    query_unit, query_factor = zip(*[unit_rows(part) for part in by_head(raw[0], head_dim)])
    key_unit, key_factor = zip(*[unit_rows(part) for part in by_head(raw[1], head_dim)])
    queries = jnp.concatenate(query_unit, 1).astype(jnp.bfloat16)
    keys_values = jnp.concatenate(key_unit + (raw[2],), 1).astype(jnp.bfloat16)
    all_keys_values, grad_group = exchange(
        [(keys_values, "row", None), (grad_update, "col", None)], 1
    )
    all_keys_values = all_keys_values.reshape(-1, 2 * inner)
    grad_group = grad_group.reshape(span, width)
    grad_attended = dot_rows(grad_group, out_weight).astype(jnp.bfloat16)
    attended, grad_query, key_part, value_part = attention(
        attn_scale, queries, all_keys_values, grad_attended
    )
    update_part = jnp.dot(attended, out_weight, preferred_element_type=jnp.float32).astype(
        jnp.bfloat16
    )
    out_part = dot_columns(attended, grad_group).astype(jnp.bfloat16)
    key_slots, value_slots, update_slots = exchange(
        [(key_part, "row", 0), (value_part, "row", 0), (update_part, "col", 0)], 2
    )
    update = add_up(update_slots).astype(jnp.bfloat16)

    def raw_grads(grad_unit, unit, factor):
        parts = zip(by_head(grad_unit, head_dim), unit, factor)
        return jnp.concatenate([unit_grad(*part) for part in parts], 1).astype(jnp.bfloat16)

    grad_raw = [
        raw_grads(grad_query, query_unit, query_factor),
        raw_grads(add_up(key_slots), key_unit, key_factor),
        add_up(value_slots).astype(jnp.bfloat16),
    ]
    qkv_part = jnp.stack([dot_columns(group, part).astype(jnp.bfloat16) for part in grad_raw])
    hidden_part = (
        sum(dot_rows(part, qkv_weight[k]) for k, part in enumerate(grad_raw))
    ).astype(jnp.bfloat16)
    qkv_slots, hidden_slots, out_slots = exchange(
        [(qkv_part, "row", 1), (hidden_part, "col", 0), (out_part, "row", 1)], 3
    )
    grad_qkv = add_up(qkv_slots)
    grad_out = add_up(out_slots)
    grad_normed = add_up(hidden_slots) * gain
    grad_tokens = (
        rstd * (grad_normed - normed * jnp.mean(grad_normed * normed, -1, keepdims=True))
    ).astype(jnp.bfloat16)
    return (update, grad_tokens, grad_qkv, grad_out)


def solution(mesh):
    placed = (
        P(("row", "col"), None),
        P(),
        P(),
        P(None, None, "col"),
        P("col"),
        P("col", None),
        P(("row", "col"), None),
    )
    return jax.shard_map(
        per_device,
        mesh=mesh,
        in_specs=placed,
        out_specs=(
            P(("row", "col"), None),
            P(("row", "col"), None),
            P(None, "row", "col"),
            P("col", "row"),
        ),
        check_vma=False,
    )
```

time: 424 us -> 269 us (0.63)
  Pallas kernels: 0 us -> 229 us
  waiting for transfers between devices: 202 us -> 0 us
  matrix products: 109 us -> 14.2 us
  local copies, waits for them, and re-layouts: 50.9 us -> 4.32 us
  blocking collectives: 26.4 us -> 0 us
  between operations: 15.3 us -> 1.8 us
    pallas_call x0 -> x5, Pallas kernels: none -> 229 us  [the longest x4 218 us: exchange(): pl.pallas_call(functools.partial(exchange_kernel, tuple(plan)), out_shape...]
    reduce_scatter x4 -> x0, waiting for transfers between devices: 130 us -> none  [the longest x1 59.7 us: per_device(): lax.psum_scatter(qkv_part.astype(jnp.bfloat16), 'row', scatter_dimension=...]
    dot_general x34 -> x12, matrix products: 109 us -> 14.2 us  [the longest x4 5.02 us: dot_rows(): lax.dot_general(left, right, (((1,), (1,)), ((), ())), preferred_element_...]
    all_gather x6 -> x0, waiting for transfers between devices: 70.8 us -> none  [the longest x1 30.6 us: per_device(): group = lax.all_gather(hidden, 'col', axis=0, tiled=True)]
    all_gather x2 -> x0, blocking collectives: 26.4 us -> none  [the longest x1 13.2 us: per_device(): lax.all_gather(inverse.T, 'row', axis=0, tiled=True)]
    unnamed x30 -> x44, local copies, waits for them, and re-layouts: 15.4 us -> 4.32 us
    dynamic_slice x8 -> x0, local copies, waits for them, and re-layouts: 8 us -> none  [per_device(): lax.scan(attend_step, carry, (split_blocks(key_piece, size), split_blocks...]
    reduce_sum x0 -> x6, other arithmetic: none -> 7.94 us  [add_up(): return jnp.sum(slots.astype(jnp.float32), 0)]
  transfers between devices with their start and end apart: 10 -> 0, of which waited for: 6 -> 0; matrix products, arithmetic and copies ran while one was open for 39% -> 0% of each run, Pallas kernels for 0% -> 0%
where the time goes in v1:
time: 269 us; the launch traced here: 268 us
  Pallas kernels  229 us (85%)
  other arithmetic  18.6 us (7%)
  matrix products  14.2 us (5%)
  local copies, waits for them, and re-layouts  4.32 us (2%)
    pallas_call x4, Pallas kernels, exchange(): pl.pallas_call(functools.partial(exchange_kernel, tuple(plan)), out_shape...  218 us
    pallas_call x1, Pallas kernels, attention(): pl.pallas_call(attention_kernel, grid=(heads, span // size), out_shape=[j...  11.7 us
    reduce_sum x6, other arithmetic, add_up(): return jnp.sum(slots.astype(jnp.float32), 0)  7.94 us

profile of v1, /device:TPU:0, one launch (start us, length us, event | category | flops | bytes accessed | tf_op | source)
XLA Modules:
  0.0 268.3 jit_solution(7825562147365643305)
XLA Ops:
  0.6 0.0 copy-start
  0.6 0.0 copy-start.10
  1.4 1.1 fusion.27
  2.5 0.0 copy-start.20
  2.5 0.1 fusion.32
  2.6 0.0 copy-start.12
  2.6 2.0 multiply_reduce_fusion
  4.6 0.0 copy-done.10
  4.6 0.1 fusion.22.refs_0_
  4.7 27.1 %exchange_0.1 = bf16[8,64,2048]{2,1,0:T(8,128)(2,1)S(1)} custom-call(bf16[64,2048]{1,0:T(8,128)(2,1)S(1)} %fusion.22.refs_0_), custom_call_target="tpu_custom_call" | custom-call | tf_op jit(solution)/shard_map/exchange_0/pallas_call | solution.py:147
  31.8 0.0 copy-done.20
  31.8 0.0 copy-start.2
  31.9 0.0 copy-done.12
  31.9 0.7 convolution_convert_fusion.6
  32.6 0.7 fusion.7
  33.3 0.2 multiply_reduce_fusion.6
  33.6 0.2 fusion.30
  33.8 0.0 copy-start.7
  33.8 0.7 fusion.11
  34.5 0.0 copy-done.8
  34.6 0.2 multiply_reduce_fusion.8
  34.8 0.2 fusion.28
  35.0 0.7 pad_maximum_fusion.2.q_ref
  35.7 41.1 %exchange_1.1 = (bf16[4,512,512]{2,1,0:T(8,128)(2,1)S(1)}, bf16[8,64,2048]{2,1,0:T(8,128)(2,1)S(1)}) custom-call(bf16[512,512]{1,0:T(8,128)(2,1)S(1)} %pad_maximum_fusion.1.refs_0_, bf16[64,2048]{1,0:T(8,128)(2,1)S(1)} %copy-done.7), custom_call_target="tpu_custom_call" | custom-call | tf_op jit(solution)/shard_map/exchange_1/pallas_call | solution.py:147
  76.8 1.3 copy-done.1
  78.1 1.5 convolution_convert_fusion.5.g_ref
  79.6 11.7 %attention.1 = (bf16[512,256]{1,0:T(8,128)(2,1)}, f32[512,256]{1,0:T(8,128)}, bf16[2048,256]{1,0:T(8,128)(2,1)}, bf16[2048,256]{1,0:T(8,128)(2,1)}) custom-call(f32[2]{0:T(128)} %scale_ref.1, bf16[512,256]{1,0:T(8,128)(2,1)} %pad_maximum_fusion.2.q_ref, bf16[2048,512]{1,0:T(8,128)(2,1)} %bitcast.39, bf16[2048,512]{1,0:T(8,128)(2,1)} %bitcast.40, ...), custom_call_target="tpu_custom_call" | custom-call | tf_op jit(solution)/shard_map/attention/pallas_call | solution.py:225
  91.3 1.7 convolution_convert_fusion.1.refs_2_
  93.0 0.4 multiply_reduce_fusion.4
  93.4 0.3 multiply_convert_fusion.3
  93.8 0.0 copy-start.18
  93.8 0.0 copy-done.2
  93.8 0.0 copy-start.17
  93.8 1.8 fusion
  95.6 0.0 copy-done.17
  95.6 2.0 convolution_convert_fusion.refs_2_
  97.6 0.0 copy-done.6
  97.6 51.3 %exchange_2.1 = (bf16[4,512,256]{2,1,0:T(8,128)(2,1)S(1)}, bf16[4,512,256]{2,1,0:T(8,128)(2,1)S(1)}, bf16[8,64,2048]{2,1,0:T(8,128)(2,1)}) custom-call(bf16[2048,256]{1,0:T(8,128)(2,1)S(1)} %copy-done.5, bf16[2048,256]{1,0:T(8,128)(2,1)S(1)} %copy-done.6, bf16[512,2048]{1,0:T(8,128)(2,1)} %convolution_convert_fusion.refs_2_), custom_call_target="tpu_custom_call" | custom-call | tf_op jit(solution)/shard_map/exchange_2/pallas_call | solution.py:147
  149.0 0.0 copy-start.4
  149.0 1.0 copy-done.4
  149.9 2.7 %reduce_sum.165 = bf16[64,2048]{1,0:T(8,128)(2,1)} reduce(bf16[8,64,2048]{2,1,0:T(8,128)(2,1)} %get-tuple-element.21, bf16[]{:T(256)} %constant.28.clone.1), dimensions={0}, to_apply=%region_6.0 | reduce | flops 917504 | bytes 2359298 | tf_op jit(solution)/shard_map/reduce_sum | solution.py:245
  152.7 2.1 reduce_sum.171
  154.8 0.1 convert_reduce_fusion.3
  155.0 1.5 multiply_reduce_fusion.2
  156.5 0.3 multiply_convert_fusion.1
  156.9 0.0 copy-start.15
  156.9 0.8 fusion.1
  157.7 0.2 copy-done.15
  157.8 0.8 fusion.2
  158.6 0.5 copy-done.16
  159.1 2.0 pad_maximum_fusion.refs_0_
  161.1 1.0 copy-done.13
  162.1 0.7 fusion.5
  162.8 0.2 copy-done.19
  163.0 0.7 fusion.9
  163.7 2.1 add_convert_fusion.refs_1_
  165.8 98.2 %exchange_3.1 = (bf16[4,3,512,256]{3,2,1,0:T(8,128)(2,1)}, bf16[8,64,2048]{2,1,0:T(8,128)(2,1)S(1)}, bf16[4,256,512]{2,1,0:T(8,128)(2,1)S(1)}) custom-call(bf16[3,2048,256]{2,1,0:T(8,128)(2,1)} %pad_maximum_fusion.refs_0_, bf16[512,2048]{1,0:T(8,128)(2,1)} %add_convert_fusion.refs_1_, bf16[256,2048]{1,0:T(8,128)(2,1)S(1)} %convolution_convert_fusion.1.refs_2_), custom_call_target="tpu_custom_call" | custom-call | tf_op jit(solution)/shard_map/exchange_3/pallas_call | solution.py:147
  264.1 0.3 convert_reduce_fusion.1
  264.4 0.2 copy-done.21
  264.6 0.2 fusion.23
  264.9 0.9 fusion.26
  265.8 0.9 convert_reduce_fusion.2
  266.7 0.0 copy-done.11
  266.7 1.6 convert_reduce_fusion
  (32 shorter events, 0.1 us)
Async XLA Ops:
  0.6 77.5 %copy-start = (bf16[256,2048]{1,0:T(8,128)(2,1)S(1)}, bf16[256,2048]{1,0:T(8,128)(2,1)}, u32[]{:S(2)}) copy-start(bf16[256,2048]{1,0:T(8,128)(2,1)} %param.12) | copy-start | bytes 3145732
  0.6 3.9 %copy-start.10 = (bf16[64,2048]{1,0:T(8,128)(2,1)S(1)}, bf16[64,2048]{1,0:T(8,128)(2,1)}, u32[]{:S(2)}) copy-start(bf16[64,2048]{1,0:T(8,128)(2,1)} %param.7) | copy-start | bytes 786436
  2.5 29.3 %copy-start.20 = (f32[64]{0:T(128)}, f32[64]{0:T(128)S(1)}, u32[]{:S(2)}) copy-start(f32[64]{0:T(128)S(1)} %add_rsqrt_fusion.4) | copy-start | bytes 772
  2.6 29.3 %copy-start.12 = (bf16[3,2048,256]{2,1,0:T(8,128)(2,1)S(1)}, bf16[3,2048,256]{2,1,0:T(8,128)(2,1)}, u32[]{:S(2)}) copy-start(bf16[3,2048,256]{2,1,0:T(8,128)(2,1)} %param.10) | copy-start | bytes 9437188
  31.8 62.0 %copy-start.2 = (bf16[8,64,2048]{2,1,0:T(8,128)(2,1)}, bf16[8,64,2048]{2,1,0:T(8,128)(2,1)S(1)}, u32[]{:S(2)}) copy-start(bf16[8,64,2048]{2,1,0:T(8,128)(2,1)S(1)} %exchange_0.1) | copy-start | bytes 6291460
  33.3 1.2 copy-start.8
  33.8 1.9 copy-start.7
  76.8 1.3 copy-start.1
  91.3 1.7 copy-start.14
  93.8 1.8 copy-start.18
  93.8 1.8 copy-start.17
  95.6 2.0 copy-start.5
  95.6 2.0 copy-start.6
  149.0 1.0 copy-start.4
  154.8 1.7 copy-start.9
  154.8 2.1 copy-start.3
  156.9 1.0 copy-start.15
  157.8 1.2 copy-start.16
  159.1 3.0 %copy-start.13 = (bf16[3,2048,256]{2,1,0:T(8,128)(2,1)S(1)}, bf16[3,2048,256]{2,1,0:T(8,128)(2,1)}, u32[]{:S(2)}) copy-start(bf16[3,2048,256]{2,1,0:T(8,128)(2,1)} %param.10) | copy-start | bytes 9437188
  162.1 0.9 copy-start.19
  264.1 0.6 copy-start.21
  264.6 2.1 copy-start.11

commit v2 on v1

--- a/solution.py
+++ b/solution.py
@@ -35,7 +35,9 @@
 
 def piece(ref, dim, size, index):
     start = index * size
-    if dim == len(ref.shape) - 1:
+    if isinstance(start, int):
+        pass
+    elif dim == len(ref.shape) - 1:
         start = pl.multiple_of(start, 128)
     elif dim == len(ref.shape) - 2:
         start = pl.multiple_of(start, 16)
@@ -75,20 +77,11 @@
         return copy
 
     copies, hops = [], {}
-    relayed = [job for job in range(count) if plan[job][1] == RELAYED]
-    for job in relayed:
-        axis, n, dim, size = plan[job]
-        if dim is None:
-            continue
-        me = lax.axis_index(axis)
-        right, left = lax.rem(me + 1, n), lax.rem(me + 3, n)
-        opposite = piece(sources[job], dim, size, lax.rem(me + 2, n))
-        first = send(job, 4, half(opposite, 0), relays[job].at[0], right)
-        second = send(job, 5, half(opposite, 1), relays[job].at[1], left)
-        hops[job] = (first, second)
+    chained = [job for job in range(count) if plan[job][1] == RELAYED and plan[job][2] is not None]
+    relayed = [job for job in range(count) if plan[job][1] == RELAYED and job not in chained]
     for step in range(1, max(sizes.values())):
         for job, (axis, n, dim, size) in enumerate(plan):
-            if step >= n or (n == RELAYED and step == 2):
+            if step >= n or job in chained or (n == RELAYED and step == 2):
                 continue
             me = lax.axis_index(axis)
             peer = lax.rem(me + step, n)
@@ -100,6 +93,8 @@
             else:
                 copies.append(copy)
     for job, (axis, n, dim, size) in enumerate(plan):
+        if job in chained:
+            continue
         me = lax.axis_index(axis)
         source = sources[job]
         copy = pltpu.make_async_copy(
@@ -117,8 +112,61 @@
             onward, origin = (right, left) if side == 0 else (left, right)
             hops[job][side].wait_recv()
             landing = half(targets[job].at[origin], side)
-            source = landing if dim is None else relays[job].at[side]
-            copies.append(send(job, 6 + side, source, landing, onward))
+            copies.append(send(job, 6 + side, landing, landing, onward))
+    def link(job, way, owner, source):
+        axis = plan[job][0]
+        me = lax.axis_index(axis)
+        slot = owner - 1 if way == 0 else owner
+        return pltpu.make_async_remote_copy(
+            src_ref=relays[job].at[way, slot] if source is None else source,
+            dst_ref=relays[job].at[way, slot],
+            send_sem=send_sem.at[job, 3 * way + slot],
+            recv_sem=recv_sem.at[job, 3 * way + slot],
+            device_id={axis: lax.rem(me + (1 if way == 0 else RELAYED - 1), RELAYED)},
+            device_id_type=MESH,
+        )
+
+    def forward(job, way, owner, place):
+        axis, n, dim, size = plan[job]
+        mine = piece(sources[job], dim, size, owner)
+
+        @pl.when(lax.axis_index(axis) == place)
+        def _():
+            if place == (0 if way == 0 else n - 1):
+                link(job, way, owner, mine).start()
+            else:
+                copy = link(job, way, owner, None)
+                copy.wait_recv()
+                inbox = relays[job].at[way, owner - 1 if way == 0 else owner]
+                total = inbox[...].astype(jnp.float32) + mine[...].astype(jnp.float32)
+                inbox[...] = total.astype(inbox.dtype)
+                copy.start()
+
+    order = [(0, 3, 0), (1, 0, 3), (0, 2, 0), (1, 1, 3), (0, 1, 0), (1, 2, 3)]
+    order += [(0, 3, 1), (1, 0, 2), (0, 2, 1), (1, 1, 2), (0, 3, 2), (1, 0, 1)]
+    for way, owner, place in order:
+        for job in chained:
+            forward(job, way, owner, place)
+    for job in chained:
+        axis, n, dim, size = plan[job]
+        for owner in range(n):
+
+            @pl.when(lax.axis_index(axis) == owner)
+            def _():
+                total = piece(sources[job], dim, size, owner)[...].astype(jnp.float32)
+                if owner > 0:
+                    link(job, 0, owner, None).wait_recv()
+                    total = total + relays[job][0, owner - 1].astype(jnp.float32)
+                if owner < n - 1:
+                    link(job, 1, owner, None).wait_recv()
+                    total = total + relays[job][1, owner].astype(jnp.float32)
+                targets[job][0] = total
+                for other in range(n):
+                    if other > owner:
+                        link(job, 0, other, None).wait_send()
+                    if other < owner:
+                        link(job, 1, other, None).wait_send()
+
     for job in relayed:
         for copy in hops[job]:
             copy.wait_send()
@@ -135,12 +183,12 @@
         if dim is not None:
             size = block[dim] = block[dim] // n
         plan.append((axis, n, dim, size))
-        shapes.append(jax.ShapeDtypeStruct((n,) + tuple(block), array.dtype))
         if n == RELAYED and dim is not None:
-            block[-2] //= 2
+            shapes.append(jax.ShapeDtypeStruct((1,) + tuple(block), jnp.float32))
+            relays.append(pltpu.VMEM((2, n - 1) + tuple(block), array.dtype))
         else:
-            block = [16, 128]
-        relays.append(pltpu.VMEM((2,) + tuple(block), array.dtype))
+            shapes.append(jax.ShapeDtypeStruct((n,) + tuple(block), array.dtype))
+            relays.append(pltpu.VMEM((16, 128), array.dtype))
     most = max(2 * RELAYED, max(n for axis, n, dim, size in plan))
     count = len(jobs)
     in_vmem = pl.BlockSpec(memory_space=pltpu.VMEM)

time: 269 us -> 234 us (0.87)
  Pallas kernels: 229 us -> 196 us
  other arithmetic: 18.6 us -> 14.7 us
    pallas_call x4, Pallas kernels: 218 us -> 185 us  [exchange(): pl.pallas_call(functools.partial(exchange_kernel, tuple(plan)), out_shape...]
    reduce_sum x6 -> x2, other arithmetic: 7.94 us -> 3.08 us  [add_up(): return jnp.sum(slots.astype(jnp.float32), 0)]
    unnamed x44 -> x40, local copies, waits for them, and re-layouts: 4.32 us -> 6.45 us
where the time goes in v2:
time: 234 us
  Pallas kernels  196 us (84%)
  other arithmetic  14.7 us (6%)
  matrix products  14.2 us (6%)
  local copies, waits for them, and re-layouts  6.45 us (3%)
    pallas_call x4, Pallas kernels, exchange(): pl.pallas_call(functools.partial(exchange_kernel, tuple(plan)), out_shape...  185 us
    pallas_call x1, Pallas kernels, attention(): pl.pallas_call(attention_kernel, grid=(heads, span // size), out_shape=[j...  11.7 us
    unnamed x40, local copies, waits for them, and re-layouts  6.45 us
    dot_general x4, matrix products, dot_rows(): lax.dot_general(left, right, (((1,), (1,)), ((), ())), preferred_element_...  5.04 us
    dot_general x4, matrix products, dot_columns(): lax.dot_general(left, right, (((0,), (0,)), ((), ())), preferred_element_...  5.03 us

profile of v2, /device:TPU:0, one launch (start us, length us, event | category | flops | bytes accessed | tf_op | source)
XLA Modules:
  0.0 233.7 jit_solution(14060379106294128959)
XLA Ops:
  0.6 0.0 copy-start
  0.6 0.0 copy-start.9
  1.4 1.1 fusion.27
  2.5 0.0 copy-start.17
  2.5 0.1 fusion.36
  2.6 0.0 copy-start.10
  2.6 2.0 multiply_reduce_fusion
  4.6 0.0 copy-done.9
  4.6 0.1 fusion.22.refs_0_
  4.7 27.1 %exchange_0.1 = bf16[8,64,2048]{2,1,0:T(8,128)(2,1)S(1)} custom-call(bf16[64,2048]{1,0:T(8,128)(2,1)S(1)} %fusion.22.refs_0_), custom_call_target="tpu_custom_call" | custom-call | tf_op jit(solution)/shard_map/exchange_0/pallas_call | solution.py:195
  31.8 0.0 copy-done.17
  31.8 0.0 copy-start.3
  31.9 0.0 copy-done.10
  31.9 0.7 convolution_convert_fusion.6
  32.6 0.7 fusion.7
  33.3 0.0 copy-start.8
  33.3 0.2 multiply_reduce_fusion.6
  33.6 0.2 fusion.32
  33.8 0.0 copy-start.7
  33.8 0.7 fusion.11
  34.6 0.0 copy-done.8
  34.6 0.2 multiply_reduce_fusion.8
  34.8 0.2 fusion.30
  35.0 0.7 pad_maximum_fusion.2.q_ref
  35.7 0.0 copy-done.7
  35.7 41.1 %exchange_1.1 = (bf16[4,512,512]{2,1,0:T(8,128)(2,1)S(1)}, bf16[8,64,2048]{2,1,0:T(8,128)(2,1)S(1)}) custom-call(bf16[512,512]{1,0:T(8,128)(2,1)S(1)} %pad_maximum_fusion.1.refs_0_, bf16[64,2048]{1,0:T(8,128)(2,1)S(1)} %copy-done.7), custom_call_target="tpu_custom_call" | custom-call | tf_op jit(solution)/shard_map/exchange_1/pallas_call | solution.py:195
  76.8 0.0 copy-start.1
  76.8 1.3 copy-done.1
  78.1 0.0 copy-done
  78.1 1.5 convolution_convert_fusion.5.g_ref
  79.6 11.7 %attention.1 = (bf16[512,256]{1,0:T(8,128)(2,1)}, f32[512,256]{1,0:T(8,128)}, bf16[2048,256]{1,0:T(8,128)(2,1)}, bf16[2048,256]{1,0:T(8,128)(2,1)}) custom-call(f32[2]{0:T(128)} %scale_ref.1, bf16[512,256]{1,0:T(8,128)(2,1)} %pad_maximum_fusion.2.q_ref, bf16[2048,512]{1,0:T(8,128)(2,1)} %bitcast.45, bf16[2048,512]{1,0:T(8,128)(2,1)} %bitcast.46, ...), custom_call_target="tpu_custom_call" | custom-call | tf_op jit(solution)/shard_map/attention/pallas_call | solution.py:273
  91.3 1.7 convolution_convert_fusion.1.refs_2_
  93.0 0.0 copy-done.12
  93.0 0.4 multiply_reduce_fusion.4
  93.4 0.3 multiply_convert_fusion.3
  93.8 0.0 copy-start.15
  93.8 0.0 copy-done.3
  93.8 0.0 copy-start.14
  93.8 1.7 fusion
  95.6 0.0 copy-done.15
  95.6 0.0 copy-done.14
  95.6 2.0 convolution_convert_fusion.refs_2_
  97.6 0.0 copy-done.6
  97.6 40.7 %exchange_2.1 = (f32[1,512,256]{2,1,0:T(8,128)S(1)}, f32[1,512,256]{2,1,0:T(8,128)S(1)}, bf16[8,64,2048]{2,1,0:T(8,128)(2,1)S(1)}) custom-call(bf16[2048,256]{1,0:T(8,128)(2,1)S(1)} %copy-done.5, bf16[2048,256]{1,0:T(8,128)(2,1)S(1)} %copy-done.6, bf16[512,2048]{1,0:T(8,128)(2,1)} %convolution_convert_fusion.refs_2_), custom_call_target="tpu_custom_call" | custom-call | tf_op jit(solution)/shard_map/exchange_2/pallas_call | solution.py:195
  138.3 1.3 copy-done.2
  139.6 2.7 %reduce_sum.148 = bf16[64,2048]{1,0:T(8,128)(2,1)} reduce(bf16[8,64,2048]{2,1,0:T(8,128)(2,1)} %copy-done.2, bf16[]{:T(256)} %constant.27.clone.1), dimensions={0}, to_apply=%region_6.0 | reduce | flops 917504 | bytes 2359298 | tf_op jit(solution)/shard_map/reduce_sum | solution.py:293
  142.3 1.5 multiply_reduce_fusion.2
  143.9 1.4 multiply_convert_fusion.1
  145.3 0.8 fusion.1
  146.0 0.8 fusion.2
  146.8 0.4 copy-done.13
  147.3 2.0 pad_maximum_fusion.refs_0_
  149.3 1.0 copy-done.11
  150.3 0.7 fusion.5
  151.0 0.2 copy-done.16
  151.2 0.7 fusion.9
  151.9 2.1 add_convert_fusion.refs_1_
  154.0 75.9 %exchange_3.1 = (f32[1,3,512,256]{3,2,1,0:T(8,128)S(1)}, bf16[8,64,2048]{2,1,0:T(8,128)(2,1)S(1)}, f32[1,256,512]{2,1,0:T(8,128)S(1)}) custom-call(bf16[3,2048,256]{2,1,0:T(8,128)(2,1)} %pad_maximum_fusion.refs_0_, bf16[512,2048]{1,0:T(8,128)(2,1)} %add_convert_fusion.refs_1_, bf16[256,2048]{1,0:T(8,128)(2,1)S(1)} %convolution_convert_fusion.1.refs_2_), custom_call_target="tpu_custom_call" | custom-call | tf_op jit(solution)/shard_map/exchange_3/pallas_call | solution.py:195
  230.0 0.3 convert_reduce_fusion
  230.4 0.3 copy-done.18
  230.6 0.2 fusion.23
  230.9 0.9 fusion.26
  231.7 1.1 copy.22
  232.9 0.8 copy.23
  (24 shorter events, 0.1 us)
Async XLA Ops:
  0.6 77.5 %copy-start = (bf16[256,2048]{1,0:T(8,128)(2,1)S(1)}, bf16[256,2048]{1,0:T(8,128)(2,1)}, u32[]{:S(2)}) copy-start(bf16[256,2048]{1,0:T(8,128)(2,1)} %param.12) | copy-start | bytes 3145732
  0.6 3.9 %copy-start.9 = (bf16[64,2048]{1,0:T(8,128)(2,1)S(1)}, bf16[64,2048]{1,0:T(8,128)(2,1)}, u32[]{:S(2)}) copy-start(bf16[64,2048]{1,0:T(8,128)(2,1)} %param.7) | copy-start | bytes 786436
  2.5 29.3 %copy-start.17 = (f32[64]{0:T(128)}, f32[64]{0:T(128)S(1)}, u32[]{:S(2)}) copy-start(f32[64]{0:T(128)S(1)} %add_rsqrt_fusion.4) | copy-start | bytes 772
  2.6 29.3 %copy-start.10 = (bf16[3,2048,256]{2,1,0:T(8,128)(2,1)S(1)}, bf16[3,2048,256]{2,1,0:T(8,128)(2,1)}, u32[]{:S(2)}) copy-start(bf16[3,2048,256]{2,1,0:T(8,128)(2,1)} %param.10) | copy-start | bytes 9437188
  31.8 61.9 %copy-start.3 = (bf16[8,64,2048]{2,1,0:T(8,128)(2,1)}, bf16[8,64,2048]{2,1,0:T(8,128)(2,1)S(1)}, u32[]{:S(2)}) copy-start(bf16[8,64,2048]{2,1,0:T(8,128)(2,1)S(1)} %exchange_0.1) | copy-start | bytes 6291460
  33.3 1.2 copy-start.8
  33.8 1.9 copy-start.7
  76.8 1.3 copy-start.1
  91.3 1.7 copy-start.12
  93.8 1.8 copy-start.15
  93.8 1.8 copy-start.14
  95.6 2.0 copy-start.5
  95.6 2.0 copy-start.6
  138.3 1.3 copy-start.2
  142.3 2.9 %copy-start.4 = (bf16[8,64,2048]{2,1,0:T(8,128)(2,1)S(1)}, bf16[8,64,2048]{2,1,0:T(8,128)(2,1)}, u32[]{:S(2)}) copy-start(bf16[8,64,2048]{2,1,0:T(8,128)(2,1)} %copy-done.3) | copy-start | bytes 6291460
  146.0 1.2 copy-start.13
  147.2 3.0 %copy-start.11 = (bf16[3,2048,256]{2,1,0:T(8,128)(2,1)S(1)}, bf16[3,2048,256]{2,1,0:T(8,128)(2,1)}, u32[]{:S(2)}) copy-start(bf16[3,2048,256]{2,1,0:T(8,128)(2,1)} %param.10) | copy-start | bytes 9437188
  150.3 0.9 copy-start.16
  230.0 0.6 copy-start.18
